TPU v7x, 32 devices: a whole 2x2x4 slice. The times are simulated.
32 devices in a mesh: gx: 4 (over z), gy: 4 (over x, core), gz: 2 (over y).
Axes of the slice: x: 2, y: 2, z: 4, core: 2. Of those that a mesh axis runs over, the one named last changes fastest.
Arguments:
- blocks: bfloat16 [4, 4, 128, 256, 256], P('gy', 'gx'), may hold values from -0.0625 to 0.0625
- block_rows: int32 [4, 4, 128], P('gy', 'gx'), may hold values from 0 to 15
- block_cols: int32 [4, 4, 128], P('gy', 'gx'), may hold values from 0 to 15
- probe_bits: int32 [16384, 256], P(('gy', 'gx'), 'gz'), may hold values from 0 to 1
- shift: float32 [16384], P(('gy', 'gx')), may hold values from 0 to 0.7
Outputs:
- forms: float32 [3, 256], P(None, 'gz')
- last_term: float32 [16384, 256], P(('gy', 'gx'), 'gz')
All inputs are finite; a program needn't handle non-finite values.
Results may differ from a plain program's by a relative error of at most 0.02.
Values may be sent and summed in bfloat16 or wider, within the bound.
No kernel may reach another device: no remote copies, remote signals or barrier semaphores. Data moves between devices by JAX's collectives and lax.ppermute only.
A program may use at most 128 MiB of HBM per device.

v0:
```python
import jax
import jax.numpy as jnp
from jax import lax
from jax.sharding import PartitionSpec as P


def body(blocks, block_rows, block_cols, probe_bits, shift):
    tile_blocks = blocks[0, 0]
    rows_here = block_rows[0, 0]
    cols_here = block_cols[0, 0]
    block_size = tile_blocks.shape[1]
    local_rows = shift.shape[0]
    probe_count = probe_bits.shape[1]
    tile_rows = local_rows // block_size * lax.axis_size("gx")
    signs = (2 * probe_bits - 1).astype(jnp.float32)

    def apply_operator(field):
        rounded = field.astype(jnp.bfloat16)
        whole = lax.all_gather(rounded, "gy", axis=0, tiled=True)
        whole = whole.reshape(whole.shape[0] // block_size, block_size, probe_count)
        picked = whole[cols_here]
        product = jnp.einsum(
            "kab,kbp->kap", tile_blocks, picked, preferred_element_type=jnp.float32
        )
        partial_rows = (
            jnp.zeros((tile_rows, block_size, probe_count), jnp.float32).at[rows_here].add(product)
        )
        summed = lax.psum_scatter(
            partial_rows.reshape(lax.axis_size("gx") * local_rows, probe_count).astype(
                jnp.bfloat16
            ),
            "gx",
            scatter_dimension=0,
            tiled=True,
        ).astype(jnp.float32)
        return summed + shift[:, None] * field

    first = apply_operator(signs)
    second = 2.0 * apply_operator(first) - signs
    third = 2.0 * apply_operator(second) - first
    forms = jnp.stack(
        [lax.psum(jnp.sum(signs * term, axis=0), ("gx", "gy")) for term in (first, second, third)]
    )
    return (forms, third)


def solution(mesh):
    return jax.shard_map(
        body,
        mesh=mesh,
        in_specs=(
            P("gy", "gx", None, None, None),
            P("gy", "gx", None),
            P("gy", "gx", None),
            P(("gy", "gx"), "gz"),
            P(("gy", "gx")),
        ),
        out_specs=(P(None, "gz"), P(("gy", "gx"), "gz")),
        check_vma=False,
    )
```

profile of v0, /device:TPU:0, one launch (start us, length us, event | category | flops | bytes accessed | tf_op | source)
XLA Modules:
  0.0 390.7 jit_solution(4236453247020909070)
XLA Ops:
  7.2 0.0 all-gather.4.cloned.1.call-start
  7.2 1.8 convert_convert_fusion
  9.0 0.0 all-gather.4.cloned.1.call-update
  9.1 0.0 reduce-scatter.4.cloned.1.call-start
  9.1 0.7 fusion.18
  9.8 0.7 fusion.17
  10.4 19.1 %all-gather.4.cloned.1.call-done = bf16[4096,128]{1,0:T(8,128)(2,1)} async-done(((bf16[1024,128]{1,0:T(8,128)(2,1)}), bf16[4096,128]{1,0:T(8,128)(2,1)}) %all-gather.4.cloned.1.call-update) | async-done | bytes 1048592 | tf_op jit(solution)/shard_map/all_gather | solution.py:19
  29.6 7.8 %gather_fusion = bf16[128,256,128]{2,1,0:T(8,128)(2,1)} fusion(bf16[16,256,128]{2,1,0:T(8,128)(2,1)} %bitcast.39, s32[1024]{0:T(1024)S(1)} %pad_clamp_fusion), kind=kCustom, calls=%fused_computation | custom fusion | bytes 16777728 | tf_op jit(solution)/shard_map/gather | solution.py:21
  37.3 17.2 %fusion.6 = f32[128,256,128]{1,2,0:T(8,128)} fusion(bf16[128,256,128]{2,1,0:T(8,128)(2,1)} %gather_fusion, bf16[1,1,128,256,256]{4,3,2,1,0:T(8,128)(2,1)} %param.5), kind=kOutput, calls=%fused_computation.12 | convolution fusion | flops 2147483648 | bytes 41943040 | tf_op jit(solution)/shard_map/kab,kbp->kap/dot_general | solution.py:22
  54.5 17.4 %copy.11 = f32[128,256,128]{2,1,0:T(8,128)} copy(f32[128,256,128]{1,2,0:T(8,128)} %fusion.6) | data formatting | bytes 33554432 | tf_op jit(solution)/shard_map/kab,kbp->kap/dot_general | solution.py:22
  71.9 0.2 broadcast.45.clone
  72.1 0.0 copy-start
  72.1 0.0 copy-start.3
  72.1 24.3 %scatter_fusion = f32[16,256,128]{2,1,0:T(8,128)S(1)} fusion(f32[16,256,128]{2,1,0:T(8,128)S(1)} %broadcast.45.clone, s32[128]{0:T(128)S(1)} %fusion.17, f32[128,256,128]{2,1,0:T(8,128)} %copy.11), kind=kCustom, calls=%fused_computation.3 | custom fusion | flops 4194304 | bytes 50332160 | tf_op jit(solution)/shard_map/scatter-add | solution.py:26
  96.5 1.2 convert_element_type.41
  97.7 0.0 reduce-scatter.4.cloned.1.call-update
  97.7 0.0 all-gather.6.cloned.1.call-start
  97.7 27.4 %reduce-scatter.4.cloned.1.call-done = bf16[1024,128]{1,0:T(8,128)(2,1)} async-done(((bf16[4096,128]{1,0:T(8,128)(2,1)}), bf16[1024,128]{1,0:T(8,128)(2,1)}) %reduce-scatter.4.cloned.1.call-update) | async-done | bytes 262160 | tf_op jit(solution)/shard_map/reduce_scatter | solution.py:28
  125.1 0.0 copy-done
  125.1 0.0 copy-done.3
  125.1 1.9 fusion.15
  127.0 0.0 all-gather.6.cloned.1.call-update
  127.0 0.0 reduce-scatter.6.cloned.1.call-start
  127.0 15.5 %all-gather.6.cloned.1.call-done = bf16[4096,128]{1,0:T(8,128)(2,1)} async-done(((bf16[1024,128]{1,0:T(8,128)(2,1)}), bf16[4096,128]{1,0:T(8,128)(2,1)}) %all-gather.6.cloned.1.call-update) | async-done | bytes 1048592 | tf_op jit(solution)/shard_map/all_gather | solution.py:19
  142.5 7.8 %gather_fusion.1 = bf16[128,256,128]{2,1,0:T(8,128)(2,1)} fusion(bf16[16,256,128]{2,1,0:T(8,128)(2,1)} %bitcast.41, s32[1024]{0:T(1024)S(1)} %pad_clamp_fusion), kind=kCustom, calls=%fused_computation.1 | custom fusion | bytes 16777728 | tf_op jit(solution)/shard_map/gather | solution.py:21
  150.3 17.2 %fusion.9 = f32[128,256,128]{1,2,0:T(8,128)} fusion(bf16[128,256,128]{2,1,0:T(8,128)(2,1)} %gather_fusion.1, bf16[1,1,128,256,256]{4,3,2,1,0:T(8,128)(2,1)} %param.5), kind=kOutput, calls=%fused_computation.13 | convolution fusion | flops 2147483648 | bytes 41943040 | tf_op jit(solution)/shard_map/kab,kbp->kap/dot_general | solution.py:22
  167.4 17.4 %copy.13 = f32[128,256,128]{2,1,0:T(8,128)} copy(f32[128,256,128]{1,2,0:T(8,128)} %fusion.9) | data formatting | bytes 33554432 | tf_op jit(solution)/shard_map/kab,kbp->kap/dot_general | solution.py:22
  184.8 0.2 broadcast.45.clone.1
  185.1 0.0 copy-start.1
  185.1 24.3 %scatter_fusion.1 = f32[16,256,128]{2,1,0:T(8,128)S(1)} fusion(f32[16,256,128]{2,1,0:T(8,128)S(1)} %broadcast.45.clone.1, s32[128]{0:T(128)S(1)} %fusion.17, f32[128,256,128]{2,1,0:T(8,128)} %copy.13), kind=kCustom, calls=%fused_computation.4 | custom fusion | flops 4194304 | bytes 50332160 | tf_op jit(solution)/shard_map/scatter-add | solution.py:26
  209.4 1.2 convert_element_type.45
  210.6 0.0 reduce-scatter.6.cloned.1.call-update
  210.6 0.0 all-gather.8.cloned.1.call-start
  210.6 27.4 %reduce-scatter.6.cloned.1.call-done = bf16[1024,128]{1,0:T(8,128)(2,1)} async-done(((bf16[4096,128]{1,0:T(8,128)(2,1)}), bf16[1024,128]{1,0:T(8,128)(2,1)}) %reduce-scatter.6.cloned.1.call-update) | async-done | bytes 262160 | tf_op jit(solution)/shard_map/reduce_scatter | solution.py:28
  238.0 0.0 copy-done.1
  238.0 1.9 fusion.16
  239.9 0.0 all-gather.8.cloned.1.call-update
  240.0 0.2 reduce-scatter.8.cloned.1.call-start
  240.2 15.1 %all-gather.8.cloned.1.call-done = bf16[4096,128]{1,0:T(8,128)(2,1)} async-done(((bf16[1024,128]{1,0:T(8,128)(2,1)}), bf16[4096,128]{1,0:T(8,128)(2,1)}) %all-gather.8.cloned.1.call-update) | async-done | bytes 1048592 | tf_op jit(solution)/shard_map/all_gather | solution.py:19
  255.3 7.8 %gather_fusion.2 = bf16[128,256,128]{2,1,0:T(8,128)(2,1)} fusion(bf16[16,256,128]{2,1,0:T(8,128)(2,1)} %bitcast.40, s32[1024]{0:T(1024)S(1)} %pad_clamp_fusion), kind=kCustom, calls=%fused_computation.2 | custom fusion | bytes 16777728 | tf_op jit(solution)/shard_map/gather | solution.py:21
  263.1 17.2 %fusion.12 = f32[128,256,128]{1,2,0:T(8,128)} fusion(bf16[128,256,128]{2,1,0:T(8,128)(2,1)} %gather_fusion.2, bf16[1,1,128,256,256]{4,3,2,1,0:T(8,128)(2,1)} %param.5), kind=kOutput, calls=%fused_computation.14 | convolution fusion | flops 2147483648 | bytes 41943040 | tf_op jit(solution)/shard_map/kab,kbp->kap/dot_general | solution.py:22
  280.3 17.4 %copy.15 = f32[128,256,128]{2,1,0:T(8,128)} copy(f32[128,256,128]{1,2,0:T(8,128)} %fusion.12) | data formatting | bytes 33554432 | tf_op jit(solution)/shard_map/kab,kbp->kap/dot_general | solution.py:22
  297.7 0.2 broadcast.45
  297.9 0.0 copy-start.2
  297.9 24.3 %scatter_fusion.2 = f32[16,256,128]{2,1,0:T(8,128)S(1)} fusion(f32[16,256,128]{2,1,0:T(8,128)S(1)} %broadcast.45, s32[128]{0:T(128)S(1)} %fusion.17, f32[128,256,128]{2,1,0:T(8,128)} %copy.15), kind=kCustom, calls=%fused_computation.5 | custom fusion | flops 4194304 | bytes 50332160 | tf_op jit(solution)/shard_map/scatter-add | solution.py:26
  322.2 1.2 convert_element_type.49
  323.4 0.0 reduce-scatter.8.cloned.1.call-update
  323.4 27.4 %reduce-scatter.8.cloned.1.call-done = bf16[1024,128]{1,0:T(8,128)(2,1)} async-done(((bf16[4096,128]{1,0:T(8,128)(2,1)}), bf16[1024,128]{1,0:T(8,128)(2,1)}) %reduce-scatter.8.cloned.1.call-update) | async-done | bytes 262160 | tf_op jit(solution)/shard_map/reduce_scatter | solution.py:28
  350.9 0.0 copy-done.2
  350.9 2.2 multiply_reduce_fusion.2
  353.0 30.2 %all-reduce = (f32[1,128]{1,0:T(1,128)S(1)}, f32[1,128]{1,0:T(1,128)S(1)}, f32[1,128]{1,0:T(1,128)S(1)}) all-reduce(f32[1,128]{1,0:T(1,128)S(1)} %bitcast.47, f32[1,128]{1,0:T(1,128)S(1)} %bitcast.46, f32[1,128]{1,0:T(1,128)S(1)} %bitcast.45), channel_id=1, replica_groups=mesh['gx'=4,'gy'=4,'gz'=2] {'gx','gy'}, use_global_device_ids=true, to_apply=%region_11.0 | all-reduce | flops 384 | bytes 3072 | tf_op jit(solution)/shard_map/psum | solution.py:42
  383.3 0.6 pad_maximum_fusion
  (1 shorter events, 0.0 us)
Async XLA Ops:
  7.2 22.4 %all-gather.4.cloned.1.call-start = ((), (), s32[]{:S(2)}) async-start(), calls=%async_computation.3 | async-start | bytes 1310720 | tf_op jit(solution)/shard_map/all_gather | solution.py:19
  9.1 116.0 %reduce-scatter.4.cloned.1.call-start = ((), (), s32[]{:S(2)}) async-start(), calls=%async_computation.4 | async-start | bytes 1310720 | tf_op jit(solution)/shard_map/reduce_scatter | solution.py:28
  72.1 53.0 %copy-start = (s32[1024,128]{1,0:T(8,128)S(1)}, s32[1024,128]{1,0:T(8,128)}, u32[]{:S(2)}) copy-start(s32[1024,128]{1,0:T(8,128)} %param.8) | copy-start | bytes 1572868
  72.1 53.0 %copy-start.3 = (f32[1024]{0:T(1024)S(1)}, f32[1024]{0:T(1024)}, u32[]{:S(2)}) copy-start(f32[1024]{0:T(1024)} %param.9) | copy-start | bytes 12292
  97.7 44.8 %all-gather.6.cloned.1.call-start = ((), (), s32[]{:S(2)}) async-start(), calls=%async_computation.5 | async-start | bytes 1310720 | tf_op jit(solution)/shard_map/all_gather | solution.py:19
  127.0 111.0 %reduce-scatter.6.cloned.1.call-start = ((), (), s32[]{:S(2)}) async-start(), calls=%async_computation.6 | async-start | bytes 1310720 | tf_op jit(solution)/shard_map/reduce_scatter | solution.py:28
  185.1 53.0 %copy-start.1 = (bf16[1024,128]{1,0:T(8,128)(2,1)S(1)}, bf16[1024,128]{1,0:T(8,128)(2,1)}, u32[]{:S(2)}) copy-start(bf16[1024,128]{1,0:T(8,128)(2,1)} %reduce-scatter.4.cloned.1.call-done) | copy-start | bytes 786436
  210.6 44.7 %all-gather.8.cloned.1.call-start = ((), (), s32[]{:S(2)}) async-start(), calls=%async_computation.7 | async-start | bytes 1310720 | tf_op jit(solution)/shard_map/all_gather | solution.py:19
  240.0 110.9 %reduce-scatter.8.cloned.1.call-start = ((), (), s32[]{:S(2)}) async-start(), calls=%async_computation.8 | async-start | bytes 1310720 | tf_op jit(solution)/shard_map/reduce_scatter | solution.py:28
  297.9 53.0 %copy-start.2 = (bf16[1024,128]{1,0:T(8,128)(2,1)S(1)}, bf16[1024,128]{1,0:T(8,128)(2,1)}, u32[]{:S(2)}) copy-start(bf16[1024,128]{1,0:T(8,128)(2,1)} %reduce-scatter.6.cloned.1.call-done) | copy-start | bytes 786436
Sparse Core Ops, SparseCore 0:
  10.1 19.4 all-gather.3
  97.8 27.2 reduce-scatter.3
  127.2 15.2 all-gather.5
  210.7 27.2 reduce-scatter.5
  240.1 15.1 all-gather.7
  323.6 27.2 reduce-scatter.7
where the time goes:
time: 393 us; the launch traced here: 391 us
  waiting for transfers between devices  132 us (34%)
  other arithmetic  86.2 us (22%)
  local copies, waits for them, and re-layouts  76.1 us (19%)
  matrix products  51.5 us (13%)
  blocking collectives  30.2 us (8%)
  between operations  14.2 us (4%)
    reduce_scatter x3, waiting for transfers between devices, apply_operator(): lax.psum_scatter(partial_rows.reshape(lax.axis_size('gx') * local_rows, p...  82.1 us
    scatter-add x3, other arithmetic, apply_operator(): jnp.zeros((tile_rows, block_size, probe_count), jnp.float32).at[rows_here]  73 us
    dot_general x3, local copies, waits for them, and re-layouts, apply_operator(): jnp.einsum('kab,kbp->kap', tile_blocks, picked, preferred_element_type=jn...  52.2 us
    dot_general x3, matrix products, apply_operator(): jnp.einsum('kab,kbp->kap', tile_blocks, picked, preferred_element_type=jn...  51.5 us
    all_gather x3, waiting for transfers between devices, apply_operator(): whole = lax.all_gather(rounded, 'gy', axis=0, tiled=True)  49.7 us
    psum x1, blocking collectives, body(): lax.psum(jnp.sum(signs * term, axis=0), ('gx', 'gy'))  30.2 us
    gather x3, local copies, waits for them, and re-layouts, apply_operator(): picked = whole[cols_here]  23.3 us
  transfers between devices with their start and end apart: 6, of which 6 were waited for; matrix products, arithmetic and copies ran while one was open for 0% of the time, Pallas kernels for 0%

commit v1 on v0

--- a/solution.py
+++ b/solution.py
@@ -39,7 +39,10 @@
     second = 2.0 * apply_operator(first) - signs
     third = 2.0 * apply_operator(second) - first
     forms = jnp.stack(
-        [lax.psum(jnp.sum(signs * term, axis=0), ("gx", "gy")) for term in (first, second, third)]
+        [
+            lax.psum(lax.psum(jnp.sum(signs * term, axis=0), "gx"), "gy")
+            for term in (first, second, third)
+        ]
     )
     return (forms, third)
 

time: 393 us -> 377 us (0.959)
  blocking collectives: 30.2 us -> 14.9 us
    psum x1 -> x2, blocking collectives: 30.2 us -> 14.9 us  [the longest x1 9.26 us: body(): lax.psum(jnp.sum(signs * term, axis=0), 'gx')]
where the time goes in v1:
time: 377 us; the launch traced here: 375 us
  waiting for transfers between devices  132 us (35%)
  other arithmetic  86.2 us (23%)
  local copies, waits for them, and re-layouts  76.1 us (20%)
  matrix products  51.5 us (14%)
  blocking collectives  14.9 us (4%)
  between operations  14.2 us (4%)
    reduce_scatter x3, waiting for transfers between devices, apply_operator(): lax.psum_scatter(partial_rows.reshape(lax.axis_size('gx') * local_rows, p...  82.1 us
    scatter-add x3, other arithmetic, apply_operator(): jnp.zeros((tile_rows, block_size, probe_count), jnp.float32).at[rows_here]  73 us
    dot_general x3, local copies, waits for them, and re-layouts, apply_operator(): jnp.einsum('kab,kbp->kap', tile_blocks, picked, preferred_element_type=jn...  52.2 us
    dot_general x3, matrix products, apply_operator(): jnp.einsum('kab,kbp->kap', tile_blocks, picked, preferred_element_type=jn...  51.5 us
    all_gather x3, waiting for transfers between devices, apply_operator(): whole = lax.all_gather(rounded, 'gy', axis=0, tiled=True)  49.7 us
    gather x3, local copies, waits for them, and re-layouts, apply_operator(): picked = whole[cols_here]  23.3 us
    psum x1, blocking collectives, body(): lax.psum(jnp.sum(signs * term, axis=0), 'gx')  9.26 us
  transfers between devices with their start and end apart: 6, of which 6 were waited for; matrix products, arithmetic and copies ran while one was open for 0% of the time, Pallas kernels for 0%

profile of v1, /device:TPU:0, one launch (start us, length us, event | category | flops | bytes accessed | tf_op | source)
XLA Modules:
  0.0 375.4 jit_solution(10025132262927477808)
XLA Ops:
  7.2 0.0 all-gather.4.cloned.1.call-start
  7.2 1.8 convert_convert_fusion
  9.0 0.0 all-gather.4.cloned.1.call-update
  9.1 0.0 reduce-scatter.4.cloned.1.call-start
  9.1 0.7 fusion.18
  9.8 0.7 fusion.17
  10.4 19.1 %all-gather.4.cloned.1.call-done = bf16[4096,128]{1,0:T(8,128)(2,1)} async-done(((bf16[1024,128]{1,0:T(8,128)(2,1)}), bf16[4096,128]{1,0:T(8,128)(2,1)}) %all-gather.4.cloned.1.call-update) | async-done | bytes 1048592 | tf_op jit(solution)/shard_map/all_gather | solution.py:19
  29.6 7.8 %gather_fusion = bf16[128,256,128]{2,1,0:T(8,128)(2,1)} fusion(bf16[16,256,128]{2,1,0:T(8,128)(2,1)} %bitcast.39, s32[1024]{0:T(1024)S(1)} %pad_clamp_fusion), kind=kCustom, calls=%fused_computation | custom fusion | bytes 16777728 | tf_op jit(solution)/shard_map/gather | solution.py:21
  37.3 17.2 %fusion.6 = f32[128,256,128]{1,2,0:T(8,128)} fusion(bf16[128,256,128]{2,1,0:T(8,128)(2,1)} %gather_fusion, bf16[1,1,128,256,256]{4,3,2,1,0:T(8,128)(2,1)} %param.5), kind=kOutput, calls=%fused_computation.12 | convolution fusion | flops 2147483648 | bytes 41943040 | tf_op jit(solution)/shard_map/kab,kbp->kap/dot_general | solution.py:22
  54.5 17.4 %copy.11 = f32[128,256,128]{2,1,0:T(8,128)} copy(f32[128,256,128]{1,2,0:T(8,128)} %fusion.6) | data formatting | bytes 33554432 | tf_op jit(solution)/shard_map/kab,kbp->kap/dot_general | solution.py:22
  71.9 0.2 broadcast.45.clone
  72.1 0.0 copy-start
  72.1 0.0 copy-start.3
  72.1 24.3 %scatter_fusion = f32[16,256,128]{2,1,0:T(8,128)S(1)} fusion(f32[16,256,128]{2,1,0:T(8,128)S(1)} %broadcast.45.clone, s32[128]{0:T(128)S(1)} %fusion.17, f32[128,256,128]{2,1,0:T(8,128)} %copy.11), kind=kCustom, calls=%fused_computation.3 | custom fusion | flops 4194304 | bytes 50332160 | tf_op jit(solution)/shard_map/scatter-add | solution.py:26
  96.5 1.2 convert_element_type.41
  97.7 0.0 reduce-scatter.4.cloned.1.call-update
  97.7 0.0 all-gather.6.cloned.1.call-start
  97.7 27.4 %reduce-scatter.4.cloned.1.call-done = bf16[1024,128]{1,0:T(8,128)(2,1)} async-done(((bf16[4096,128]{1,0:T(8,128)(2,1)}), bf16[1024,128]{1,0:T(8,128)(2,1)}) %reduce-scatter.4.cloned.1.call-update) | async-done | bytes 262160 | tf_op jit(solution)/shard_map/reduce_scatter | solution.py:28
  125.1 0.0 copy-done
  125.1 0.0 copy-done.3
  125.1 1.9 fusion.15
  127.0 0.0 all-gather.6.cloned.1.call-update
  127.0 0.0 reduce-scatter.6.cloned.1.call-start
  127.0 15.5 %all-gather.6.cloned.1.call-done = bf16[4096,128]{1,0:T(8,128)(2,1)} async-done(((bf16[1024,128]{1,0:T(8,128)(2,1)}), bf16[4096,128]{1,0:T(8,128)(2,1)}) %all-gather.6.cloned.1.call-update) | async-done | bytes 1048592 | tf_op jit(solution)/shard_map/all_gather | solution.py:19
  142.5 7.8 %gather_fusion.1 = bf16[128,256,128]{2,1,0:T(8,128)(2,1)} fusion(bf16[16,256,128]{2,1,0:T(8,128)(2,1)} %bitcast.41, s32[1024]{0:T(1024)S(1)} %pad_clamp_fusion), kind=kCustom, calls=%fused_computation.1 | custom fusion | bytes 16777728 | tf_op jit(solution)/shard_map/gather | solution.py:21
  150.3 17.2 %fusion.9 = f32[128,256,128]{1,2,0:T(8,128)} fusion(bf16[128,256,128]{2,1,0:T(8,128)(2,1)} %gather_fusion.1, bf16[1,1,128,256,256]{4,3,2,1,0:T(8,128)(2,1)} %param.5), kind=kOutput, calls=%fused_computation.13 | convolution fusion | flops 2147483648 | bytes 41943040 | tf_op jit(solution)/shard_map/kab,kbp->kap/dot_general | solution.py:22
  167.4 17.4 %copy.13 = f32[128,256,128]{2,1,0:T(8,128)} copy(f32[128,256,128]{1,2,0:T(8,128)} %fusion.9) | data formatting | bytes 33554432 | tf_op jit(solution)/shard_map/kab,kbp->kap/dot_general | solution.py:22
  184.8 0.2 broadcast.45.clone.1
  185.1 0.0 copy-start.1
  185.1 24.3 %scatter_fusion.1 = f32[16,256,128]{2,1,0:T(8,128)S(1)} fusion(f32[16,256,128]{2,1,0:T(8,128)S(1)} %broadcast.45.clone.1, s32[128]{0:T(128)S(1)} %fusion.17, f32[128,256,128]{2,1,0:T(8,128)} %copy.13), kind=kCustom, calls=%fused_computation.4 | custom fusion | flops 4194304 | bytes 50332160 | tf_op jit(solution)/shard_map/scatter-add | solution.py:26
  209.4 1.2 convert_element_type.45
  210.6 0.0 reduce-scatter.6.cloned.1.call-update
  210.6 0.0 all-gather.8.cloned.1.call-start
  210.6 27.4 %reduce-scatter.6.cloned.1.call-done = bf16[1024,128]{1,0:T(8,128)(2,1)} async-done(((bf16[4096,128]{1,0:T(8,128)(2,1)}), bf16[1024,128]{1,0:T(8,128)(2,1)}) %reduce-scatter.6.cloned.1.call-update) | async-done | bytes 262160 | tf_op jit(solution)/shard_map/reduce_scatter | solution.py:28
  238.0 0.0 copy-done.1
  238.0 1.9 fusion.16
  239.9 0.0 all-gather.8.cloned.1.call-update
  240.0 0.2 reduce-scatter.8.cloned.1.call-start
  240.2 15.1 %all-gather.8.cloned.1.call-done = bf16[4096,128]{1,0:T(8,128)(2,1)} async-done(((bf16[1024,128]{1,0:T(8,128)(2,1)}), bf16[4096,128]{1,0:T(8,128)(2,1)}) %all-gather.8.cloned.1.call-update) | async-done | bytes 1048592 | tf_op jit(solution)/shard_map/all_gather | solution.py:19
  255.3 7.8 %gather_fusion.2 = bf16[128,256,128]{2,1,0:T(8,128)(2,1)} fusion(bf16[16,256,128]{2,1,0:T(8,128)(2,1)} %bitcast.40, s32[1024]{0:T(1024)S(1)} %pad_clamp_fusion), kind=kCustom, calls=%fused_computation.2 | custom fusion | bytes 16777728 | tf_op jit(solution)/shard_map/gather | solution.py:21
  263.1 17.2 %fusion.12 = f32[128,256,128]{1,2,0:T(8,128)} fusion(bf16[128,256,128]{2,1,0:T(8,128)(2,1)} %gather_fusion.2, bf16[1,1,128,256,256]{4,3,2,1,0:T(8,128)(2,1)} %param.5), kind=kOutput, calls=%fused_computation.14 | convolution fusion | flops 2147483648 | bytes 41943040 | tf_op jit(solution)/shard_map/kab,kbp->kap/dot_general | solution.py:22
  280.3 17.4 %copy.15 = f32[128,256,128]{2,1,0:T(8,128)} copy(f32[128,256,128]{1,2,0:T(8,128)} %fusion.12) | data formatting | bytes 33554432 | tf_op jit(solution)/shard_map/kab,kbp->kap/dot_general | solution.py:22
  297.7 0.2 broadcast.45
  297.9 0.0 copy-start.2
  297.9 24.3 %scatter_fusion.2 = f32[16,256,128]{2,1,0:T(8,128)S(1)} fusion(f32[16,256,128]{2,1,0:T(8,128)S(1)} %broadcast.45, s32[128]{0:T(128)S(1)} %fusion.17, f32[128,256,128]{2,1,0:T(8,128)} %copy.15), kind=kCustom, calls=%fused_computation.5 | custom fusion | flops 4194304 | bytes 50332160 | tf_op jit(solution)/shard_map/scatter-add | solution.py:26
  322.2 1.2 convert_element_type.49
  323.4 0.0 reduce-scatter.8.cloned.1.call-update
  323.4 27.4 %reduce-scatter.8.cloned.1.call-done = bf16[1024,128]{1,0:T(8,128)(2,1)} async-done(((bf16[4096,128]{1,0:T(8,128)(2,1)}), bf16[1024,128]{1,0:T(8,128)(2,1)}) %reduce-scatter.8.cloned.1.call-update) | async-done | bytes 262160 | tf_op jit(solution)/shard_map/reduce_scatter | solution.py:28
  350.9 0.0 copy-done.2
  350.9 2.2 multiply_reduce_fusion.2
  353.0 9.3 %all-reduce.1 = (f32[128]{0:T(128)S(1)}, f32[128]{0:T(128)S(1)}, f32[128]{0:T(128)S(1)}) all-reduce(f32[128]{0:T(128)S(1)} %get-tuple-element.4, f32[128]{0:T(128)S(1)} %get-tuple-element.3, f32[128]{0:T(128)S(1)} %get-tuple-element.2), channel_id=1, replica_groups=mesh['gx'=4,'gy'=4,'gz'=2] {'gx'}, use_global_device_ids=true, to_apply=%region_13.0 | all-reduce | flops 384 | bytes 3072 | tf_op jit(solution)/shard_map/psum | solution.py:43
  362.3 5.7 %all-reduce = (f32[1,128]{1,0:T(1,128)S(1)}, f32[1,128]{1,0:T(1,128)S(1)}, f32[1,128]{1,0:T(1,128)S(1)}) all-reduce(f32[1,128]{1,0:T(1,128)S(1)} %bitcast.45, f32[1,128]{1,0:T(1,128)S(1)} %bitcast.46, f32[1,128]{1,0:T(1,128)S(1)} %bitcast.47), channel_id=1, replica_groups=mesh['gx'=4,'gy'=4,'gz'=2] {'gy'}, use_global_device_ids=true, to_apply=%region_14.0 | all-reduce | flops 384 | bytes 3072 | tf_op jit(solution)/shard_map/psum | solution.py:43
  368.0 0.6 pad_maximum_fusion
  (1 shorter events, 0.0 us)
Async XLA Ops:
  7.2 22.4 %all-gather.4.cloned.1.call-start = ((), (), s32[]{:S(2)}) async-start(), calls=%async_computation.3 | async-start | bytes 1310720 | tf_op jit(solution)/shard_map/all_gather | solution.py:19
  9.1 116.0 %reduce-scatter.4.cloned.1.call-start = ((), (), s32[]{:S(2)}) async-start(), calls=%async_computation.4 | async-start | bytes 1310720 | tf_op jit(solution)/shard_map/reduce_scatter | solution.py:28
  72.1 53.0 %copy-start = (s32[1024,128]{1,0:T(8,128)S(1)}, s32[1024,128]{1,0:T(8,128)}, u32[]{:S(2)}) copy-start(s32[1024,128]{1,0:T(8,128)} %param.8) | copy-start | bytes 1572868
  72.1 53.0 %copy-start.3 = (f32[1024]{0:T(1024)S(1)}, f32[1024]{0:T(1024)}, u32[]{:S(2)}) copy-start(f32[1024]{0:T(1024)} %param.9) | copy-start | bytes 12292
  97.7 44.8 %all-gather.6.cloned.1.call-start = ((), (), s32[]{:S(2)}) async-start(), calls=%async_computation.5 | async-start | bytes 1310720 | tf_op jit(solution)/shard_map/all_gather | solution.py:19
  127.0 111.0 %reduce-scatter.6.cloned.1.call-start = ((), (), s32[]{:S(2)}) async-start(), calls=%async_computation.6 | async-start | bytes 1310720 | tf_op jit(solution)/shard_map/reduce_scatter | solution.py:28
  185.1 53.0 %copy-start.1 = (bf16[1024,128]{1,0:T(8,128)(2,1)S(1)}, bf16[1024,128]{1,0:T(8,128)(2,1)}, u32[]{:S(2)}) copy-start(bf16[1024,128]{1,0:T(8,128)(2,1)} %reduce-scatter.4.cloned.1.call-done) | copy-start | bytes 786436
  210.6 44.7 %all-gather.8.cloned.1.call-start = ((), (), s32[]{:S(2)}) async-start(), calls=%async_computation.7 | async-start | bytes 1310720 | tf_op jit(solution)/shard_map/all_gather | solution.py:19
  240.0 110.9 %reduce-scatter.8.cloned.1.call-start = ((), (), s32[]{:S(2)}) async-start(), calls=%async_computation.8 | async-start | bytes 1310720 | tf_op jit(solution)/shard_map/reduce_scatter | solution.py:28
  297.9 53.0 %copy-start.2 = (bf16[1024,128]{1,0:T(8,128)(2,1)S(1)}, bf16[1024,128]{1,0:T(8,128)(2,1)}, u32[]{:S(2)}) copy-start(bf16[1024,128]{1,0:T(8,128)(2,1)} %reduce-scatter.6.cloned.1.call-done) | copy-start | bytes 786436
Sparse Core Ops, SparseCore 0:
  10.1 19.4 all-gather.3
  97.8 27.2 reduce-scatter.3
  127.2 15.2 all-gather.5
  210.7 27.2 reduce-scatter.5
  240.1 15.1 all-gather.7
  323.6 27.2 reduce-scatter.7
